TPU v7x, 32 devices: a 4x4x1 block of a 4x4x8 slice. The times are simulated.
32 devices in a mesh: dp: 1 (over z), dcp: 32 (over y, x, core).
Axes of the slice: x: 4, y: 4, z: 1, core: 2. Of those that a mesh axis runs over, the one named last changes fastest.
The devices are a block of a 4x4x8 slice.
Arguments:
- q_abs: bfloat16 [128, 128, 576], P('dp', 'dcp')
- latent_cache: bfloat16 [128, 1, 32, 256, 576], P('dp', None, 'dcp')
- ctx_len: int32 [128], P('dp')
Outputs:
- output: bfloat16 [128, 128, 512], P(('dp', 'dcp'))
All inputs are finite; a program needn't handle non-finite values.
Results may differ from a plain program's by a relative error of at most 0.0061068.
Values are sent between devices in bfloat16 or wider.
A program may use at most 768 MiB of HBM per device.

v0:
```python
import jax
import jax.numpy as jnp
from jax import lax
from jax.sharding import PartitionSpec as P

ROPE_DIM = 64
QK_DIM = 192


def solution(mesh):
    group_size = mesh.shape['dcp']

    def local_step(q_blk, cache_blk, len_blk):
        batch_rows = q_blk.shape[0]
        num_pages = cache_blk.shape[1]
        page_len = cache_blk.shape[3]
        latent_dim = q_blk.shape[2] - ROPE_DIM
        out_rows = batch_rows // group_size
        dev_index = lax.axis_index('dcp')
        q_full = lax.all_gather(q_blk, 'dcp', axis=1, tiled=True)
        cache_own = cache_blk[:, :, 0]
        scores = jnp.einsum('bhw,bjtw->bhjt', q_full, cache_own, preferred_element_type=jnp.float32) * (QK_DIM ** -0.5)
        positions = (jnp.arange(num_pages)[:, None] * group_size + dev_index) * page_len + jnp.arange(page_len)[None, :]
        is_valid = positions[None] < len_blk[:, None, None]
        scores = jnp.where(is_valid[:, None], scores, -1e30)
        row_max = jnp.max(scores, axis=(2, 3))
        weights_exp = jnp.exp(scores - row_max[:, :, None, None])
        denom_sum = jnp.sum(weights_exp, axis=(2, 3))
        pv_sum = jnp.einsum('bhjt,bjtw->bhw', weights_exp.astype(jnp.bfloat16), cache_own, preferred_element_type=jnp.float32)
        part_out = (pv_sum[..., :latent_dim] / denom_sum[..., None]).astype(jnp.bfloat16)
        part_lse = row_max + jnp.log(denom_sum)
        recv_out = lax.all_to_all(part_out, 'dcp', 0, 0, tiled=True).reshape(group_size, out_rows, part_out.shape[1], latent_dim)
        recv_lse = lax.all_to_all(part_lse, 'dcp', 0, 0, tiled=True).reshape(group_size, out_rows, part_lse.shape[1])
        total_lse = jax.nn.logsumexp(recv_lse, axis=0)
        merge_weights = jnp.exp(recv_lse - total_lse[None])
        merged = jnp.sum(merge_weights[..., None] * recv_out.astype(jnp.float32), axis=0)
        return merged.astype(jnp.bfloat16)

    return jax.shard_map(local_step, mesh=mesh, in_specs=(P('dp', 'dcp', None), P('dp', None, 'dcp', None, None), P('dp')), out_specs=P(('dp', 'dcp'), None, None), check_vma=False)
```

profile of v0, /device:TPU:107, one launch (start us, length us, event | category | flops | bytes accessed | tf_op | source)
XLA Modules:
  0.0 422.1 jit_solution(13871584631606010784)
XLA Ops:
  6.5 0.0 all-gather.2.cloned.1.call-start
  6.6 0.7 all-gather.2.cloned.1.call-update
  7.3 0.7 broadcast_compare_fusion
  8.1 74.8 %all-gather.2.cloned.1.call-done = bf16[128,128,576]{0,2,1:T(8,128)(2,1)} async-done(((bf16[128,4,576]{0,2,1:T(8,128)(2,1)}), bf16[128,128,576]{0,2,1:T(8,128)(2,1)}) %all-gather.2.cloned.1.call-update) | async-done | bytes 18874384 | tf_op jit(solution)/shard_map/all_gather | solution.py:20
  82.9 27.9 %copy.5 = bf16[128,128,576]{2,1,0:T(8,128)(2,1)} copy(bf16[128,128,576]{0,2,1:T(8,128)(2,1)} %all-gather.2.cloned.1.call-done) | data formatting | bytes 37748736 | tf_op jit(solution)/shard_map/all_gather | solution.py:20
  110.8 27.3 %fusion.3 = (f32[128,128]{1,0:T(8,128)S(1)}, f32[128,128,256]{2,1,0:T(8,128)}) fusion(pred[128,256]{1,0:T(8,128)(4,1)S(1)} %broadcast_compare_fusion, bf16[128,128,576]{2,1,0:T(8,128)(2,1)} %copy.5, bf16[128,1,1,256,576]{3,4,2,1,0:T(8,128)(2,1)} %param.4), kind=kOutput, calls=%fused_computation.7 | convolution fusion | flops 4844404736 | bytes 73498624 | tf_op jit(solution)/shard_map/bhw,bjtw->bhjt/dot_general | solution.py:22
  138.1 8.8 %fusion.5 = f32[128,128]{1,0:T(8,128)S(1)} fusion(f32[128,128,256]{2,1,0:T(8,128)} %get-tuple-element.6, f32[128,128]{1,0:T(8,128)S(1)} %get-tuple-element.5, pred[128,256]{1,0:T(8,128)(4,1)S(1)} %broadcast_compare_fusion), kind=kLoop, calls=%fused_computation.9 | loop fusion | flops 16760832 | bytes 16941056 | tf_op jit(solution)/shard_map/reduce_sum | solution.py:28
  146.9 0.6 log_add_fusion
  147.6 5.9 %all-to-all-start = ((f32[32,4,128]{2,1,0:T(4,128)}), f32[32,4,128]{2,1,0:T(4,128)S(1)}, u32[]{:S(2)}, u32[]{:S(2)}) async-start(f32[32,4,128]{2,1,0:T(4,128)} %bitcast.1), calls=%async_computation | async-start | bytes 131072 | tf_op jit(solution)/shard_map/all_to_all | solution.py:33
  153.4 24.1 %divide_convert_fusion = bf16[128,128,512]{2,1,0:T(8,128)(2,1)} fusion(f32[128,128]{1,0:T(8,128)S(1)} %fusion.5, bf16[128,256,576]{1,2,0:T(8,128)(2,1)} %bitcast.12, f32[128,128,256]{2,1,0:T(8,128)} %get-tuple-element.6, f32[128,128]{1,0:T(8,128)S(1)} %get-tuple-element.5, pred[128,256]{1,0:T(8,128)(4,1)S(1)} %broadcast_compare_fusion), kind=kOutput, calls=%fused_computation.4 | convolution fusion | flops 4328521728 | bytes 67272704 | tf_op jit(solution)/shard_map/bhjt,bjtw->bhw/dot_general | solution.py:29
  177.5 0.0 all-to-all-done
  177.5 6.3 %all-to-all-start.1 = ((bf16[128,128,512]{2,1,0:T(8,128)(2,1)}), bf16[128,128,512]{2,1,0:T(8,128)(2,1)}, u32[]{:S(2)}, u32[]{:S(2)}) async-start(bf16[128,128,512]{2,1,0:T(8,128)(2,1)} %divide_convert_fusion), calls=%async_computation.1 | async-start | bytes 33554432 | tf_op jit(solution)/shard_map/all_to_all | solution.py:32
  183.9 0.1 exponential_reduce_fusion
  184.0 223.1 %all-to-all-done.1 = bf16[128,128,512]{2,1,0:T(8,128)(2,1)} async-done(((bf16[128,128,512]{2,1,0:T(8,128)(2,1)}), bf16[128,128,512]{2,1,0:T(8,128)(2,1)}, u32[]{:S(2)}, u32[]{:S(2)}) %all-to-all-start.1) | async-done | bytes 16777248 | tf_op jit(solution)/shard_map/all_to_all | solution.py:32
  407.1 8.1 %fusion.2 = bf16[4,128,512]{2,1,0:T(8,128)(2,1)} fusion(bf16[32,4,128,512]{3,2,1,0:T(8,128)(2,1)} %bitcast.3, f32[32,4,128]{2,1,0:T(4,128)S(1)} %bitcast.14), kind=kLoop, calls=%fused_computation.3 | loop fusion | flops 24903680 | bytes 17367040 | tf_op jit(solution)/shard_map/reduce_sum | solution.py:36
  (6 shorter events, 0.1 us)
Async XLA Ops:
  6.5 76.3 %all-gather.2.cloned.1.call-start = ((), (), s32[]{:S(2)}) async-start(), calls=%async_computation.2 | async-start | bytes 19464192 | tf_op jit(solution)/shard_map/all_gather | solution.py:20
  147.6 30.0 %all-to-all-start = ((f32[32,4,128]{2,1,0:T(4,128)}), f32[32,4,128]{2,1,0:T(4,128)S(1)}, u32[]{:S(2)}, u32[]{:S(2)}) async-start(f32[32,4,128]{2,1,0:T(4,128)} %bitcast.1), calls=%async_computation | async-start | bytes 131072 | tf_op jit(solution)/shard_map/all_to_all | solution.py:33
  177.5 229.6 %all-to-all-start.1 = ((bf16[128,128,512]{2,1,0:T(8,128)(2,1)}), bf16[128,128,512]{2,1,0:T(8,128)(2,1)}, u32[]{:S(2)}, u32[]{:S(2)}) async-start(bf16[128,128,512]{2,1,0:T(8,128)(2,1)} %divide_convert_fusion), calls=%async_computation.1 | async-start | bytes 33554432 | tf_op jit(solution)/shard_map/all_to_all | solution.py:32
Sparse Core Ops, SparseCore 0:
  9.4 73.4 all-gather.1
where the time goes:
time: 423 us; the launch traced here: 422 us
  waiting for transfers between devices  299 us (71%)
  matrix products  51.4 us (12%)
  local copies, waits for them, and re-layouts  27.9 us (7%)
  other arithmetic  18.4 us (4%)
  between operations  13.5 us (3%)
  starting transfers between devices  12.2 us (3%)
    all_to_all x1, waiting for transfers between devices, local_step(): lax.all_to_all(part_out, 'dcp', 0, 0, tiled=True)  223 us
    all_gather x1, waiting for transfers between devices, local_step(): q_full = lax.all_gather(q_blk, 'dcp', axis=1, tiled=True)  74.8 us
    all_gather x1, local copies, waits for them, and re-layouts, local_step(): q_full = lax.all_gather(q_blk, 'dcp', axis=1, tiled=True)  27.9 us
    dot_general x1, matrix products, local_step(): jnp.einsum('bhw,bjtw->bhjt', q_full, cache_own, preferred_element_type=jn...  27.3 us
    dot_general x1, matrix products, local_step(): jnp.einsum('bhjt,bjtw->bhw', weights_exp.astype(jnp.bfloat16), cache_own,...  24.1 us
    reduce_sum x1, other arithmetic, local_step(): denom_sum = jnp.sum(weights_exp, axis=(2, 3))  8.79 us
  transfers between devices with their start and end apart: 3, of which 2 were waited for; matrix products, arithmetic and copies ran while one was open for 6% of the time, Pallas kernels for 0%

commit v1 on v0

v1 whole, which is shorter than its diff:
```python
import functools
import math

import jax
import jax.numpy as jnp
from jax import lax
from jax.experimental import pallas as pl
from jax.experimental.pallas import tpu as pltpu
from jax.sharding import PartitionSpec as P

ROPE_DIM = 64
QK_DIM = 192
AXIS = 'dcp'
DEPTH = 3
SLICES = 4

FIRST, SECOND = 0, 1
FULL, LOW, HIGH = 0, 1, 2
GATHER = (
    (FIRST, 1, (0, 0), FULL),
    (FIRST, -1, (0, 0), FULL),
    (FIRST, 1, (-1, 0), LOW),
    (FIRST, -1, (1, 0), HIGH),
    (SECOND, 1, (0, 0), FULL),
    (SECOND, 1, (-1, 0), FULL),
    (SECOND, 1, (1, 0), FULL),
    (SECOND, 1, (2, 0), LOW),
    (SECOND, 1, (2, 0), HIGH),
    (SECOND, -1, (0, 0), FULL),
    (SECOND, -1, (-1, 0), FULL),
    (SECOND, -1, (1, 0), FULL),
    (SECOND, -1, (2, 0), LOW),
    (SECOND, -1, (2, 0), HIGH),
    (SECOND, 1, (0, -1), FULL),
    (SECOND, 1, (-1, -1), FULL),
    (SECOND, -1, (1, 1), FULL),
    (SECOND, -1, (2, 1), LOW),
    (SECOND, -1, (2, 1), HIGH),
)
REDUCE = ((2, LOW, 1), (1, HIGH, 1), (2, HIGH, -1), (-1, LOW, -1), (1, LOW, 1), (-1, HIGH, -1))


def _kernel(side, len_ref, q_ref, cache_ref, out_ref, sib_ref, q_own, q_sib, q_all, part, page, xbuf, ybuf, lse_x, lse_y,
            wgt, q_sem, page_sem, swap_send, swap_recv, qs_send, qs_recv, ag_send, ag_recv, rs_send, rs_recv, ls_send,
            ls_recv):
    nj, nt, hc, width = q_own.shape
    heads = part.shape[3]
    latent = part.shape[4]
    page_len = page.shape[3]
    half_t, half_h = nt // 2, heads // 2
    quarter_t, quarter_h = nt // 4, heads // 4

    me = lax.axis_index(AXIS)
    core = lax.rem(me, 2)
    xpos = lax.rem(me // 2, side)
    ypos = me // (2 * side)
    sibling = me + 1 - 2 * core

    def wrap(pos, step):
        return lax.rem(pos + (step + side), side)

    def neighbour(axis, half, step):
        if axis == half:
            return (ypos * side + wrap(xpos, step)) * 2 + core
        return (wrap(ypos, step) * side + xpos) * 2 + core

    def peer(dev):
        return {AXIS: dev}

    def gather_copy(j, half, idx, receive=False):
        axis, step, (df, ds), rng = GATHER[idx]
        dev = neighbour(axis, half, step)
        if receive:
            if axis == FIRST:
                df -= step
            else:
                ds -= step
        if half == 0:
            yy, xx = wrap(ypos, ds), wrap(xpos, df)
        else:
            yy, xx = wrap(ypos, df), wrap(xpos, ds)
        start = half * half_t + (quarter_t if rng == HIGH else 0)
        ref = q_all.at[j, yy, xx, pl.ds(start, half_t if rng == FULL else quarter_t)]
        return pltpu.make_async_remote_copy(
            src_ref=ref, dst_ref=ref, send_sem=ag_send.at[j, half, idx], recv_sem=ag_recv.at[j, half, idx],
            device_id=peer(dev), device_id_type=pl.DeviceIdType.MESH)

    def rows_of(half, rng):
        return half * half_h + (quarter_h if rng == HIGH else 0)

    def first_part(r, half, step, rng, i=None):
        hs = pl.ds(rows_of(half, rng), quarter_h)
        second = slice(None) if i is None else i
        if half == 0:
            return part.at[r, second, wrap(xpos, step), hs]
        return part.at[r, wrap(ypos, step), second, hs]

    def second_part(r, half, step, rng):
        hs = pl.ds(rows_of(half, rng), quarter_h)
        if half == 0:
            return part.at[r, wrap(ypos, step), xpos, hs]
        return part.at[r, ypos, wrap(xpos, step), hs]

    def reduce_copy(r, half, axis, idx):
        dest, rng, step = REDUCE[idx]
        src = (first_part if axis == FIRST else second_part)(r, half, dest, rng)
        dst = (xbuf if axis == FIRST else ybuf).at[r, half, idx]
        return pltpu.make_async_remote_copy(
            src_ref=src, dst_ref=dst, send_sem=rs_send.at[r, half, axis, idx], recv_sem=rs_recv.at[r, half, axis, idx],
            device_id=peer(neighbour(axis, half, step)), device_id_type=pl.DeviceIdType.MESH)

    def lse_copy(j, axis, idx):
        buf = lse_x if axis == 0 else lse_y
        return pltpu.make_async_remote_copy(
            src_ref=buf.at[j, 0], dst_ref=buf.at[j, idx + 1], send_sem=ls_send.at[j, axis, idx],
            recv_sem=ls_recv.at[j, axis, idx], device_id=peer(neighbour(axis, 0, (1, -1, 2)[idx])),
            device_id_type=pl.DeviceIdType.MESH)

    def swap_copy(j):
        return pltpu.make_async_remote_copy(
            src_ref=cache_ref.at[:, 1 - core, j], dst_ref=sib_ref.at[j], send_sem=swap_send.at[j],
            recv_sem=swap_recv.at[j], device_id=peer(sibling), device_id_type=pl.DeviceIdType.MESH)

    def query_swap(j):
        return pltpu.make_async_remote_copy(
            src_ref=q_ref.at[:, 1 - core, j], dst_ref=q_sib.at[j], send_sem=qs_send.at[j],
            recv_sem=qs_recv.at[j], device_id=peer(sibling), device_id_type=pl.DeviceIdType.MESH)

    def query_own(j):
        return pltpu.make_async_copy(q_ref.at[:, core, j], q_own.at[j], q_sem.at[j])

    def page_copies(j, t):
        slot = lax.rem(t, DEPTH)
        return (pltpu.make_async_copy(cache_ref.at[t, core, j], page.at[slot, 0], page_sem.at[slot, 0]),
                pltpu.make_async_copy(sib_ref.at[j, t], page.at[slot, 1], page_sem.at[slot, 1]))

    def merge_queries(j):
        query_own(j).wait()
        query_swap(j).wait_recv()
        q_all[j, ypos, xpos] = q_own[j] + q_sib[j]

    def own_sends(j):
        for idx in (0, 1, 4, 9):
            for half in (0, 1):
                gather_copy(j, half, idx).start()

    def gather_events(j, events):
        for idx, sends in events:
            for half in (0, 1):
                gather_copy(j, half, idx, receive=True).wait_recv()
                for s in sends:
                    gather_copy(j, half, s).start()

    def first_pages(j):
        swap_copy(j).wait_recv()
        for t in range(DEPTH - 1):
            for c in page_copies(j, t):
                c.start()

    def attend(j, t):
        @pl.when(t + DEPTH - 1 < nt)
        def _():
            for c in page_copies(j, t + DEPTH - 1):
                c.start()

        slot = lax.rem(t, DEPTH)
        for c in page_copies(j, t):
            c.wait()
        q = q_all[j, :, :, t].reshape(heads, width)
        limit = len_ref[(t * 2 + core) * nj + j]
        outs, lses = [], []
        for p in (0, 1):
            owner = me if p == 0 else sibling
            s = jnp.dot(q, page[slot, p], preferred_element_type=jnp.float32) * (QK_DIM ** -0.5)
            position = owner * page_len + lax.broadcasted_iota(jnp.int32, (1, page_len), 1)
            s = jnp.where(position < limit, s, -1e30)
            m = jnp.max(s, axis=1, keepdims=True)
            w = jnp.exp(s - m)
            l = jnp.sum(w, axis=1, keepdims=True)
            pv = lax.dot_general(w.astype(jnp.bfloat16), page[slot, p, :latent], (((1,), (1,)), ((), ())),
                                 preferred_element_type=jnp.float32)
            outs.append((pv * (1.0 / l)).astype(jnp.bfloat16).astype(jnp.float32))
            lses.append(m + jnp.log(l))
        top = jnp.maximum(lses[0], lses[1])
        both = top + jnp.log(jnp.exp(lses[0] - top) + jnp.exp(lses[1] - top))
        part[j, t // side, lax.rem(t, side)] = jnp.exp(lses[0] - both) * outs[0] + jnp.exp(lses[1] - both) * outs[1]
        row = jnp.broadcast_to(both, (heads, 128)).T
        lse_x[j, 0, pl.ds(t, 1), :] = row[0:1]

    def attend_slice(j, n):
        per = nt // SLICES
        lax.fori_loop(n * per, (n + 1) * per, lambda t, _: (attend(j, t), 0)[1], 0)

    def combine(v):
        top = jnp.max(v, axis=0)
        return top + jnp.log(jnp.sum(jnp.exp(v - top[None]), axis=0))

    def lse_send(j, axis):
        for idx in range(3):
            lse_copy(j, axis, idx).start()

    def lse_turn(j):
        for idx in range(3):
            lse_copy(j, 0, idx).wait_recv()
        lse_y[j, 0] = combine(lse_x[j])
        lse_send(j, 1)

    def weigh(j):
        for idx in range(3):
            lse_copy(j, 1, idx).wait_recv()
        wgt[...] = jnp.exp(lse_x[j, 0] - combine(lse_y[j]))

        def body(t, _):
            w = jnp.broadcast_to(wgt[pl.ds(t, 1), :], (128, heads)).T
            yy, xx = t // side, lax.rem(t, side)
            for i in range(latent // 128):
                cols = pl.ds(i * 128, 128)
                part[j, yy, xx, :, cols] = part[j, yy, xx, :, cols] * w
            return 0

        lax.fori_loop(0, nt, body, 0)

    def reduce_start(r, axis):
        for idx in (0, 2, 1, 3):
            for half in (0, 1):
                reduce_copy(r, half, axis, idx).start()

    def reduce_turn(r, axis):
        for idx, dest, rng, nxt in ((0, 1, LOW, 4), (2, -1, HIGH, 5)):
            for half in (0, 1):
                reduce_copy(r, half, axis, idx).wait_recv()
                if axis == FIRST:
                    def body(i, _):
                        ref = first_part(r, half, dest, rng, i)
                        ref[...] = ref[...] + xbuf[r, half, idx, i]
                        return 0
                    lax.fori_loop(0, side, body, 0)
                else:
                    ref = second_part(r, half, dest, rng)
                    ref[...] = ref[...] + ybuf[r, half, idx]
                reduce_copy(r, half, axis, nxt).start()

    def reduce_end(r, axis):
        for rng, one, two in ((HIGH, 1, 5), (LOW, 3, 4)):
            for half in (0, 1):
                reduce_copy(r, half, axis, one).wait_recv()
                reduce_copy(r, half, axis, two).wait_recv()
                if axis == FIRST:
                    def body(i, _):
                        ref = first_part(r, half, 0, rng, i)
                        ref[...] = ref[...] + (xbuf[r, half, one, i] + xbuf[r, half, two, i])
                        return 0
                    lax.fori_loop(0, side, body, 0)
                else:
                    total = second_part(r, half, 0, rng)[...] + (ybuf[r, half, one] + ybuf[r, half, two])
                    out_ref[r, pl.ds(rows_of(half, rng), quarter_h)] = total.astype(out_ref.dtype)

    for j in range(nj):
        query_own(j).start()
    barrier = pltpu.get_barrier_semaphore()
    peers = [sibling] + [neighbour(axis, 0, step) for axis in (0, 1) for step in (1, -1, 2)]
    for dev in peers:
        pl.semaphore_signal(barrier, inc=1, device_id=peer(dev), device_id_type=pl.DeviceIdType.MESH)
    pl.semaphore_wait(barrier, len(peers))

    for j in range(nj):
        query_swap(j).start()
    for j in range(nj):
        swap_copy(j).start()
    merge_queries(0)
    own_sends(0)
    lax.fori_loop(1, nj, lambda j, _: (merge_queries(j), 0)[1], 0)

    def stage(k, _):
        def when(lag, fn, *args):
            pl.when((k >= lag) & (k < nj + lag))(lambda: fn(k - lag, *args))

        when(-1, own_sends)
        when(1, first_pages)
        when(0, gather_events, ((0, (2, 5, 10)), (1, (3, 6, 11))))
        when(1, attend_slice, 0)
        when(2, lse_turn)
        when(0, gather_events, ((2, (7, 12)), (3, (8, 13)), (4, (14,)), (9, ())))
        when(1, attend_slice, 1)
        when(0, gather_events, ((5, (15,)), (11, (16,)), (10, ()), (6, ())))
        when(4, reduce_turn, FIRST)
        when(5, reduce_turn, SECOND)
        when(3, weigh)
        when(3, reduce_start, FIRST)
        when(1, attend_slice, 2)
        when(0, gather_events, ((12, (17,)), (13, (18,)), (7, ()), (8, ())))
        when(1, attend_slice, 3)
        when(1, lse_send, 0)
        when(0, gather_events, ((14, ()), (15, ()), (16, ()), (17, ()), (18, ())))
        when(4, reduce_end, FIRST)
        when(4, reduce_start, SECOND)
        when(5, reduce_end, SECOND)
        return 0

    lax.fori_loop(0, nj + 5, stage, 0)

    def drain(j, _):
        swap_copy(j).wait_send()
        query_swap(j).wait_send()
        for half in (0, 1):
            for idx in range(len(GATHER)):
                gather_copy(j, half, idx).wait_send()
            for axis in (0, 1):
                for idx in range(len(REDUCE)):
                    reduce_copy(j, half, axis, idx).wait_send()
        for axis in (0, 1):
            for idx in range(3):
                lse_copy(j, axis, idx).wait_send()
        return 0

    lax.fori_loop(0, nj, drain, 0)


def solution(mesh):
    group_size = mesh.shape[AXIS]
    side = math.isqrt(group_size // 2)
    nt = side * side

    def local_step(q_blk, cache_blk, len_blk):
        batch_rows, own_heads, width = q_blk.shape
        page_len = cache_blk.shape[3]
        latent = width - ROPE_DIM
        nj = batch_rows // group_size
        hc = 2 * own_heads
        heads = hc * nt
        core = lax.rem(lax.axis_index(AXIS), 2)
        q = q_blk.reshape(nt, 2, nj, own_heads, width)
        zero = jnp.zeros_like(q)
        q = jnp.concatenate([jnp.where(core == 0, q, zero), jnp.where(core == 1, q, zero)], axis=3)
        cache = jnp.swapaxes(cache_blk.reshape(nt, 2, nj, page_len, width), 3, 4)
        any_space = pl.BlockSpec(memory_space=pl.ANY)
        dma = pltpu.SemaphoreType.DMA
        out, _ = pl.pallas_call(
            functools.partial(_kernel, side),
            out_shape=(jax.ShapeDtypeStruct((nj, heads, latent), jnp.bfloat16),
                       jax.ShapeDtypeStruct((nj, nt, width, page_len), jnp.bfloat16)),
            in_specs=[pl.BlockSpec(memory_space=pltpu.SMEM), any_space, any_space],
            out_specs=(pl.BlockSpec(memory_space=pltpu.VMEM), any_space),
            scratch_shapes=[
                pltpu.VMEM((nj, nt, hc, width), jnp.bfloat16),
                pltpu.VMEM((nj, nt, hc, width), jnp.bfloat16),
                pltpu.VMEM((nj, side, side, nt, hc, width), jnp.bfloat16),
                pltpu.VMEM((nj, side, side, heads, latent), jnp.float32),
                pltpu.VMEM((DEPTH, 2, width, page_len), jnp.bfloat16),
                pltpu.VMEM((nj, 2, len(REDUCE), side, heads // 4, latent), jnp.float32),
                pltpu.VMEM((nj, 2, len(REDUCE), heads // 4, latent), jnp.float32),
                pltpu.VMEM((nj, 4, nt, heads), jnp.float32),
                pltpu.VMEM((nj, 4, nt, heads), jnp.float32),
                pltpu.VMEM((nt, heads), jnp.float32),
                dma((nj,)), dma((DEPTH, 2)), dma((nj,)), dma((nj,)), dma((nj,)), dma((nj,)),
                dma((nj, 2, len(GATHER))), dma((nj, 2, len(GATHER))),
                dma((nj, 2, 2, len(REDUCE))), dma((nj, 2, 2, len(REDUCE))),
                dma((nj, 2, 3)), dma((nj, 2, 3)),
            ],
            compiler_params=pltpu.CompilerParams(collective_id=0, has_side_effects=True, vmem_limit_bytes=66_000_000),
        )(len_blk, q, cache)
        return out

    return jax.shard_map(local_step, mesh=mesh, in_specs=(P('dp', AXIS, None), P('dp', None, AXIS, None, None), P('dp')),
                         out_specs=P(('dp', AXIS), None, None), check_vma=False)
```

time: 423 us -> 184 us (0.43)
  the two profiles are of different devices: /device:TPU:107 before, /device:TPU:96 now
where the time goes in v1:
time: 184 us; the launch traced here: 183 us
  Pallas kernels  177 us (96%)
  local copies, waits for them, and re-layouts  3.43 us (2%)
  other arithmetic  2.89 us (2%)
    pallas_call x1, Pallas kernels, local_step(): pl.pallas_call(functools.partial(_kernel, side), out_shape=(jax.ShapeDtyp...  177 us

profile of v1, /device:TPU:96, one launch (start us, length us, event | category | flops | bytes accessed | tf_op | source)
XLA Modules:
  0.0 183.3 jit_solution(8023821559518583257)
XLA Ops:
  0.0 1.1 broadcast_select_fusion.1
  1.1 0.8 copy.4
  1.9 0.8 copy.5
  2.7 1.8 pad_maximum_fusion.q_ref
  4.5 176.9 %shard_map.37 = (bf16[4,128,512]{2,1,0:T(8,128)(2,1)}, bf16[4,16,576,256]{3,2,1,0:T(8,128)(2,1)}) custom-call(s32[128]{0:T(128)} %len_ref.1, bf16[16,2,4,8,576]{4,3,2,1,0:T(8,128)(2,1)} %pad_maximum_fusion.q_ref, bf16[16,2,4,576,256]{4,3,2,1,0:T(8,128)(2,1)} %bitcast.5), custom_call_target="tpu_custom_call" | custom-call | tf_op jit(solution)/shard_map/pallas_call | solution.py:338
  181.4 1.9 %copy.7 = bf16[4,128,512]{2,1,0:T(8,128)(2,1)} copy(bf16[4,128,512]{2,1,0:T(8,128)(2,1)} %get-tuple-element.6) | data formatting | bytes 1048576
